TPU v7x, 32 devices: a whole 2x2x4 slice. The times are simulated.
32 devices in a mesh: gx: 8 (over z, x), yz: 4 (over y, core).
Axes of the slice: x: 2, y: 2, z: 4, core: 2. Of those that a mesh axis runs over, the one named last changes fastest.
Arguments:
- state: float32 [4, 256, 192, 256], P(None, 'gx', 'yz'), may hold values from -6 to 6
- mean_flow: float32 [256, 192, 256], P('gx', 'yz'), may hold values from 0.2 to 1.2
- face_cell: int32 [6144], P(('gx', 'yz')), may hold values from 0 to 12582911, as said below
- face_normal: float32 [3, 6144], P(None, ('gx', 'yz')), may hold values from -3 to 3
- face_pos: float32 [3, 6144], P(None, ('gx', 'yz')), may hold values from -2 to 2
- observer_pos: float32 [3, 512], replicated, may hold values from 4 to 12
- time_bin: int32 [6144, 512], P(('gx', 'yz')), may hold values from 0 to 63
Outputs:
- state_next: float32 [4, 256, 192, 256], P(None, 'gx', 'yz')
- signal: float32 [512, 64], P(('gx', 'yz'))
Inputs may be any that keep to these rules, and one draw needn't show every extreme that they name: `face_cell`: face j is held by device j // 192 of gx+yz, and its cell, numbered (x 192 + y) * 256 + z, lies in that device's block of grid cells.
All inputs are finite; a program needn't handle non-finite values.
Results may differ from a plain program's by a relative error of at most 0.000084.
Values sent between devices are 32-bit elements; how exact they have to be, the bound alone decides.
A program may use at most 192 MiB of HBM per device.

v0:
```python
import functools

import numpy as np
import jax
import jax.numpy as jnp
from jax import lax
from jax.experimental import pallas as pl
from jax.experimental.pallas import tpu as pltpu
from jax.sharding import PartitionSpec as P

BINS = 64
TILE = 8
TAPS = 5

time_step = 0.25
four_pi = 4.0 * 3.141592653589793
VMEM = pltpu.VMEM
SMEM = pltpu.SMEM


def diagonals(count):
    lower = np.full(count, 1.0 / 3.0)
    upper = np.full(count, 1.0 / 3.0)
    lower[1] = lower[count - 2] = upper[1] = upper[count - 2] = 0.25
    lower[0] = upper[count - 1] = 0.0
    lower[count - 1] = upper[0] = 2.0
    return lower, upper


def stencil(count):
    rows = np.zeros((count, count))
    for i in range(2, count - 2):
        rows[i, i + 1], rows[i, i - 1] = 7.0 / 9.0, -7.0 / 9.0
        rows[i, i + 2], rows[i, i - 2] = 1.0 / 36.0, -1.0 / 36.0
    rows[0, :3] = (-2.5, 2.0, 0.5)
    rows[1, 0], rows[1, 2] = -0.75, 0.75
    rows[count - 2, count - 3], rows[count - 2, count - 1] = -0.75, 0.75
    rows[count - 1, count - 3:] = (-0.5, -2.0, 2.5)
    return rows


def dense_derivative(count):
    lower, upper = diagonals(count)
    matrix = np.eye(count) + np.diag(lower[1:], -1) + np.diag(upper[:-1], 1)
    return np.linalg.solve(matrix, stencil(count))


def x_tables(blocks, cells):
    count = blocks * cells
    lower, upper = diagonals(count)
    rows = stencil(count)
    down, pivot = np.zeros(count), np.ones(count)
    for i in range(1, count):
        down[i] = lower[i] / pivot[i - 1]
        pivot[i] = 1.0 - down[i] * upper[i - 1]
    up, pivot_up = np.zeros(count), np.ones(count)
    for i in range(count - 2, -1, -1):
        up[i] = upper[i] / pivot_up[i + 1]
        pivot_up[i] = 1.0 - up[i] * lower[i + 1]
    from_left = rows.copy()
    for i in range(1, count):
        from_left[i] -= down[i] * from_left[i - 1]
    from_right = rows.copy()
    for i in range(count - 2, -1, -1):
        from_right[i] -= up[i] * from_right[i + 1]
    weights = np.zeros((blocks, 2, cells))
    chain = np.zeros((blocks, 2))
    sweep = np.zeros((blocks, 3, cells))
    taps = np.zeros((blocks, 4, TAPS))
    ends = np.zeros((blocks, 4))
    for d in range(blocks):
        s, e = d * cells, (d + 1) * cells
        if d < blocks - 1:
            weights[d, 0] = from_left[e + 1, s:e]
            chain[d, 0] = np.prod(-down[s + 2:e + 2])
        if d > 0:
            weights[d, 1] = from_right[s - 2, s:e]
            chain[d, 1] = np.prod(-up[s - 2:e - 2])
        sweep[d, 0] = down[s:e]
        sweep[d, 1] = 1.0 / pivot[s:e]
        sweep[d, 2] = upper[s:e] / pivot[s:e]
        sweep[d, 1, -1] = 1.0 / (pivot[e - 1] + pivot_up[e - 1] - 1.0)
        taps[d, 0, 2:] = from_left[s, s:s + 3]
        taps[d, 3, :3] = from_right[e - 1, e - 3:e]
        for k in range(-2, 3):
            if 0 <= s + 1 + k:
                taps[d, 1, k + 2] = rows[s + 1, s + 1 + k]
            if e - 2 + k < count:
                taps[d, 2, k + 2] = rows[e - 2, e - 2 + k]
        ends[d, 0] = -1.0 / down[s + 1]
        ends[d, 2] = -1.0 / up[e - 2]
        if d > 0:
            ends[d, 1] = rows[s + 1, s - 1] / down[s + 1]
        if d < blocks - 1:
            ends[d, 3] = rows[e - 2, e] / up[e - 2]
    largest, hops, reach = np.abs(chain).max(), 1, np.abs(chain).max()
    while hops < blocks - 1 and reach >= np.finfo(np.float32).tiny:
        hops, reach = hops + 1, reach * largest
    edges = np.concatenate([taps.reshape(blocks, -1), ends], 1)
    return (
        weights.astype(np.float32),
        chain.astype(np.float32),
        sweep.astype(np.float32),
        edges.astype(np.float32),
        hops,
    )


def exchange_kernel(
    sizes, table_ref, state_ref, flow_ref, zhi_ref, zlo_ref,
    left_sum, left_plane, right_sum, right_plane, low_ref, high_ref, z_out,
    zrate, field, to_right, to_left, on_right, on_left, far_left, far_right,
    load_sem, store_sem, send_sem, recv_sem,
):
    blocks, groups = sizes
    _, cells, width, _ = field.shape
    block, group = lax.axis_index("gx"), lax.axis_index("yz")
    order = (0, 2, 4, 1, 3)
    crossing = (0, 2, 4)

    def weight(side, i):
        return table_ref[0, side * cells + i]

    shifts = {"gx": (1, -1, 2, -2), "yz": (1, -1)}
    place = {"gx": (block, blocks), "yz": (group, groups)}

    def there(axis, shift):
        index, count = place[axis]
        return index + shift < count if shift > 0 else index + shift >= 0

    def other(axis, shift):
        index, count = place[axis]
        return {axis: jnp.clip(index + shift, 0, count - 1)}

    loads = {}
    for f in order:
        source = flow_ref if f == 4 else state_ref.at[f]
        loads[f] = pltpu.make_async_copy(source, field.at[f], load_sem.at[f])
        loads[f].start()

    barrier = pltpu.get_barrier_semaphore()
    pairs = [(axis, shift) for axis in shifts for shift in shifts[axis]]
    for axis, shift in pairs:
        @pl.when(there(axis, shift))
        def _():
            pl.semaphore_signal(
                barrier, inc=1, device_id=other(axis, shift),
                device_id_type=pl.DeviceIdType.MESH,
            )
    present = [there(axis, shift).astype(jnp.int32) for axis, shift in pairs]
    pl.semaphore_wait(barrier, sum(present[1:], present[0]))

    sent = []

    def copy(kind, f, source, target, axis, shift):
        moved = pltpu.make_async_remote_copy(
            src_ref=source, dst_ref=target,
            send_sem=send_sem.at[kind, f], recv_sem=recv_sem.at[kind, f],
            device_id=other(axis, shift), device_id_type=pl.DeviceIdType.MESH,
        )
        sent.append((moved, axis, shift))

        @pl.when(there(axis, shift))
        def _():
            moved.start()

        return moved, axis, shift

    def arrive(entry, targets):
        moved, axis, shift = entry

        @pl.when(there(axis, -shift))
        def _():
            moved.wait_recv()

        @pl.when(jnp.logical_not(there(axis, -shift)))
        def _():
            targets[...] = jnp.zeros_like(targets)

    near, rest = {}, []
    for f in order:
        loads[f].wait()
        plane_r = copy(0, f, field.at[f, cells - 1], left_plane.at[f], "gx", 1)
        plane_l = copy(1, f, field.at[f, 0], right_plane.at[f], "gx", -1)
        rest += [(plane_r, left_plane.at[f]), (plane_l, right_plane.at[f])]
        if f in crossing:
            slot = crossing.index(f)
            rest.append((copy(
                2, f, field.at[f, :, width - TILE:width], low_ref.at[slot], "yz", 1
            ), low_ref.at[slot]))
            rest.append((copy(
                3, f, field.at[f, :, 0:TILE], high_ref.at[slot], "yz", -1
            ), high_ref.at[slot]))
        for j in range(0, width, TILE):
            total_right = weight(0, 0) * field[f, 0, j:j + TILE]
            total_left = weight(1, 0) * field[f, 0, j:j + TILE]
            for i in range(1, cells):
                value = field[f, i, j:j + TILE]
                total_right += weight(0, i) * value
                total_left += weight(1, i) * value
            to_right[f, j:j + TILE] = total_right
            to_left[f, j:j + TILE] = total_left
        near[f] = (
            copy(4, f, to_right.at[f], left_sum.at[f], "gx", 1),
            copy(5, f, to_left.at[f], right_sum.at[f], "gx", -1),
        )
    stores = []
    group_of = 4 if cells % 4 == 0 else 1
    for slot, f in enumerate((0, 3, 4)):
        def multiply(k, carry, slot=slot, f=f):
            planes = pl.ds(k * group_of, group_of)
            block = field[f, planes].reshape(group_of * width, -1)
            high = block.astype(jnp.bfloat16)
            rest = (block - high.astype(jnp.float32)).astype(jnp.bfloat16)
            out = jnp.dot(rest, zhi_ref[...], preferred_element_type=jnp.float32)
            out += jnp.dot(high, zlo_ref[...], preferred_element_type=jnp.float32)
            out += jnp.dot(high, zhi_ref[...], preferred_element_type=jnp.float32)
            zrate[slot, planes] = out.reshape(group_of, width, -1)
            return carry
        lax.fori_loop(0, cells // group_of, multiply, 0)
        stores.append(pltpu.make_async_copy(
            zrate.at[slot], z_out.at[slot], store_sem.at[slot]
        ))
        stores[-1].start()
    far = {}
    for f in order:
        arrive(near[f][0], left_sum.at[f])
        arrive(near[f][1], right_sum.at[f])
        on_right[f] = to_right[f] + table_ref[0, 5 * cells + 0] * left_sum[f]
        on_left[f] = to_left[f] + table_ref[0, 5 * cells + 1] * right_sum[f]
        far[f] = (
            copy(6, f, on_right.at[f], far_left.at[f], "gx", 2),
            copy(7, f, on_left.at[f], far_right.at[f], "gx", -2),
        )
    for f in order:
        arrive(far[f][0], far_left.at[f])
        arrive(far[f][1], far_right.at[f])
    for entry, targets in rest:
        arrive(entry, targets)
    for store in stores:
        store.wait()
    for moved, axis, shift in sent:
        @pl.when(there(axis, shift))
        def _():
            moved.wait_send()
    for f in order:
        left_sum[f] = left_sum[f] + table_ref[0, 5 * cells + 2] * far_left[f]
        right_sum[f] = right_sum[f] + table_ref[0, 5 * cells + 3] * far_right[f]


def signal_kernel(groups, count, piece_ref, out_ref, landing, send_sem, recv_sem):
    me = lax.axis_index("gx") * groups + lax.axis_index("yz")

    def partner(k):
        index = lax.rem(me + k, count)
        return {"gx": lax.div(index, groups), "yz": lax.rem(index, groups)}, index

    barrier = pltpu.get_barrier_semaphore()
    for k in range(1, count):
        pl.semaphore_signal(
            barrier, inc=1, device_id=partner(k)[0], device_id_type=pl.DeviceIdType.MESH
        )
    pl.semaphore_wait(barrier, count - 1)
    copies = []
    for k in range(1, count):
        target, index = partner(k)
        copies.append(pltpu.make_async_remote_copy(
            src_ref=piece_ref.at[index], dst_ref=landing.at[k - 1],
            send_sem=send_sem.at[k - 1], recv_sem=recv_sem.at[k - 1],
            device_id=target, device_id_type=pl.DeviceIdType.MESH,
        ))
        copies[-1].start()
    for moved in copies:
        moved.wait()
    total = piece_ref[me]
    for k in range(count - 1):
        total += landing[k]
    out_ref[...] = total


def main_kernel(
    cells, width, depth,
    row_ref, table_ref,
    state_ref, flow_ref, left_sum, left_plane, right_sum, right_plane, low_ref, high_ref,
    zrate, geometry_ref, observer_ref, bin_ref,
    next_ref, signal_ref,
    wide, swept, rate, picked,
):
    step = pl.program_id(0)
    rows = pl.ds(pl.multiple_of(step * TILE, TILE), TILE)
    window = pl.ds(pl.multiple_of(step * TILE, TILE), 3 * TILE)

    def load(f, i):
        return flow_ref[i, rows, :] if f == 4 else state_ref[f, i, rows, :]

    @pl.when(step == 0)
    def _():
        def widen(i, carry):
            for slot, f in enumerate((0, 2, 4)):
                body = flow_ref[i] if f == 4 else state_ref[f, i]
                wide[slot, i, TILE:TILE + width, :] = body
                wide[slot, i, 0:TILE, :] = low_ref[slot, i]
                wide[slot, i, TILE + width:2 * TILE + width, :] = high_ref[slot, i]
            return carry
        lax.fori_loop(0, cells, widen, 0)

    fields = range(5)

    def tap(k, position):
        return table_ref[0, 5 * cells + 4 + k * TAPS + position + 2]

    def end(k):
        return table_ref[0, 5 * cells + 4 + 4 * TAPS + k]

    def sweep(k, i):
        return table_ref[0, (2 + k) * cells + i]

    carry = []
    for f in fields:
        first = tap(0, 0) * load(f, 0) + tap(0, 1) * load(f, 1) + tap(0, 2) * load(f, 2)
        value = first + end(0) * left_sum[f] + end(1) * left_plane[f]
        swept[f, 0] = value
        second = (
            tap(1, -1) * load(f, 0) + tap(1, 0) * load(f, 1)
            + tap(1, 1) * load(f, 2) + tap(1, 2) * load(f, 3) + tap(1, -2) * left_plane[f]
        )
        value = second - sweep(0, 1) * value
        swept[f, 1] = value
        carry.append(value)

    def forward(i, carry):
        new = []
        factor = sweep(0, i)
        for f in fields:
            rhs = 7.0 / 9.0 * (load(f, i + 1) - load(f, i - 1)) + 1.0 / 36.0 * (
                load(f, i + 2) - load(f, i - 2)
            )
            value = rhs - factor * carry[f]
            swept[f, i] = value
            new.append(value)
        return tuple(new)

    carry = lax.fori_loop(2, cells - 2, forward, tuple(carry), unroll=2)
    solved = []
    n = cells
    for f in fields:
        before = (
            tap(2, -2) * load(f, n - 4) + tap(2, -1) * load(f, n - 3) + tap(2, 0) * load(f, n - 2)
            + tap(2, 1) * load(f, n - 1) + tap(2, 2) * right_plane[f]
        )
        value = before - sweep(0, n - 2) * carry[f]
        swept[f, n - 2] = value
        last = (
            tap(3, -2) * load(f, n - 3) + tap(3, -1) * load(f, n - 2) + tap(3, 0) * load(f, n - 1)
            + end(2) * right_sum[f] + end(3) * right_plane[f]
        )
        solved.append((last - sweep(0, n - 1) * value) * sweep(1, n - 1))

    def y_rate(slot, i):
        whole = wide[slot, i, window, :]

        def take(shift):
            return whole[TILE + shift:2 * TILE + shift]

        return (
            0.75 * (take(1) - take(-1))
            - 0.15 * (take(2) - take(-2))
            + 1.0 / 60.0 * (take(3) - take(-3))
        )

    def finish(i, x):
        p, u, v, w, flow = (load(f, i) for f in fields)
        rates = (
            -(flow * x[0] + x[1] + y_rate(1, i) + zrate[1, i]),
            -(flow * x[1] + u * x[4] + v * y_rate(2, i) + w * zrate[2, i] + x[0]),
            -(flow * x[2] + y_rate(0, i)),
            -(flow * x[3] + zrate[0, i]),
        )
        place = pl.ds(pl.multiple_of(i * width + step * TILE, TILE), TILE)
        for c, old in enumerate((p, u, v, w)):
            rate[c, place, :] = rates[c]
            new = old + time_step * rates[c]
            next_ref[c, i] = new
            if c == 0:
                rate[4, place, :] = new

    finish(n - 1, solved)

    def backward(k, carry):
        i = n - 2 - k
        x = tuple(
            swept[f, i] * sweep(1, i) - sweep(2, i) * carry[f] for f in fields
        )
        finish(i, x)
        return x

    lax.fori_loop(0, n - 1, backward, tuple(solved))

    @pl.when(step == pl.num_programs(0) - 1)
    def _():
        faces = picked.shape[1]

        def pick(k, carry):
            row = row_ref[0, k]
            for c in range(5):
                picked[c, pl.ds(k, 1), :] = rate[c, pl.ds(row, 1), :]
            return carry

        lax.fori_loop(0, faces, pick, 0, unroll=4)
        mask = lax.broadcasted_iota(jnp.int32, (faces, depth), 1) == geometry_ref[:, 6:7].astype(jnp.int32)
        at = [
            jnp.sum(jnp.where(mask, picked[c], 0.0), axis=1, keepdims=True) for c in range(5)
        ]
        normal = [geometry_ref[:, c:c + 1] for c in range(3)]
        normal_rate = normal[0] * at[1] + normal[1] * at[2] + normal[2] * at[3]
        offset = [observer_ref[c:c + 1, :] - geometry_ref[:, 3 + c:4 + c] for c in range(3)]
        distance = jnp.sqrt(
            offset[0] * offset[0] + offset[1] * offset[1] + offset[2] * offset[2]
        )
        normal_r = (
            normal[0] * offset[0] + normal[1] * offset[1] + normal[2] * offset[2]
        ) / distance
        contribution = (normal_rate + (at[0] + at[4] / distance) * normal_r) / (
            four_pi * distance
        )
        bins = bin_ref[...]

        def gather(b, carry):
            signal_ref[pl.ds(b, 1), :] = jnp.sum(
                jnp.where(bins == b, contribution, 0.0), axis=0, keepdims=True
            )
            return carry

        lax.fori_loop(0, BINS, gather, 0, unroll=2)


def per_device(sizes, state, mean_flow, face_cell, face_normal, face_pos, observer_pos, time_bin):
    blocks, groups = sizes
    _, cells, width, depth = state.shape
    faces, observers = time_bin.shape
    tiles = width // TILE
    block, group = lax.axis_index("gx"), lax.axis_index("yz")
    weights, chain, sweep, edges, hops = x_tables(blocks, cells)

    params = dict(vmem_limit_bytes=60 * 1024 * 1024)
    assert hops <= 3
    links = np.zeros((blocks, 1, 4), np.float32)
    links[:, 0, :2] = chain
    links[1:, 0, 2] = chain[:-1, 0]
    links[:-1, 0, 3] = chain[1:, 1]
    tables = np.concatenate(
        [part.reshape(blocks, 1, -1) for part in (weights, sweep, links, edges)], axis=2
    )
    table = lax.dynamic_index_in_dim(jnp.asarray(tables), block, 0, keepdims=False)
    plane = jax.ShapeDtypeStruct((5, width, depth), jnp.float32)
    edge = jax.ShapeDtypeStruct((3, cells, TILE, depth), jnp.float32)
    plane_spec = pl.BlockSpec((5, TILE, depth), lambda j: (0, j, 0))
    scratch_plane = VMEM((5, width, depth), jnp.float32)
    operator = dense_derivative(depth).T.astype(np.float32)
    z_high = jnp.asarray(operator).astype(jnp.bfloat16)
    z_low = (jnp.asarray(operator) - z_high.astype(jnp.float32)).astype(jnp.bfloat16)

    *received, z_rates = pl.pallas_call(
        functools.partial(exchange_kernel, sizes),
        out_shape=(plane,) * 4 + (edge,) * 2
        + (jax.ShapeDtypeStruct((3, cells, width, depth), jnp.float32),),
        in_specs=[
            pl.BlockSpec(memory_space=SMEM),
            pl.BlockSpec(memory_space=pl.ANY),
            pl.BlockSpec(memory_space=pl.ANY),
            pl.BlockSpec(memory_space=VMEM),
            pl.BlockSpec(memory_space=VMEM),
        ],
        out_specs=(pl.BlockSpec(memory_space=VMEM),) * 6 + (pl.BlockSpec(memory_space=pl.ANY),),
        scratch_shapes=[VMEM((3, cells, width, depth), jnp.float32)]
        + [VMEM((5, cells, width, depth), jnp.float32)]
        + [scratch_plane] * 6
        + [
            pltpu.SemaphoreType.DMA((5,)),
            pltpu.SemaphoreType.DMA((3,)),
            pltpu.SemaphoreType.DMA((8, 5)),
            pltpu.SemaphoreType.DMA((8, 5)),
        ],
        compiler_params=pltpu.CompilerParams(
            collective_id=0, has_side_effects=True, vmem_limit_bytes=60 * 1024 * 1024
        ),
    )(table, state, mean_flow, z_high, z_low)

    planes = width * groups
    along_x = face_cell // (planes * depth) - block * cells
    along_y = face_cell // depth % planes - group * width
    along_z = face_cell % depth
    row = (along_x * width + along_y).reshape(1, faces)

    geometry = jnp.concatenate(
        [face_normal, face_pos, along_z.astype(jnp.float32)[None]]
    ).T

    def whole(*shape):
        return pl.BlockSpec(shape, lambda j: (0,) * len(shape))

    smem = pl.BlockSpec(memory_space=SMEM)
    state_next, signal = pl.pallas_call(
        functools.partial(main_kernel, cells, width, depth),
        grid=(tiles,),
        out_shape=(
            jax.ShapeDtypeStruct(state.shape, jnp.float32),
            jax.ShapeDtypeStruct((BINS, observers), jnp.float32),
        ),
        in_specs=[
            smem, smem,
            whole(4, cells, width, depth), whole(cells, width, depth),
            plane_spec, plane_spec, plane_spec, plane_spec,
            whole(3, cells, TILE, depth), whole(3, cells, TILE, depth),
            pl.BlockSpec((3, cells, TILE, depth), lambda j: (0, 0, j, 0)),
            whole(faces, 7),
            whole(3, observers), whole(faces, observers),
        ],
        out_specs=(
            pl.BlockSpec((4, cells, TILE, depth), lambda j: (0, 0, j, 0)),
            whole(BINS, observers),
        ),
        scratch_shapes=[
            VMEM((3, cells, width + 2 * TILE, depth), jnp.float32),
            VMEM((5, cells, TILE, depth), jnp.float32),
            VMEM((5, cells * width, depth), jnp.float32),
            VMEM((5, faces, depth), jnp.float32),
        ],
        compiler_params=pltpu.CompilerParams(**params),
    )(
        row, table,
        state, mean_flow, *received,
        z_rates, geometry,
        observer_pos, time_bin,
    )
    devices = blocks * groups
    share = observers // devices
    signal = pl.pallas_call(
        functools.partial(signal_kernel, groups, devices),
        out_shape=jax.ShapeDtypeStruct((share, BINS), jnp.float32),
        in_specs=[pl.BlockSpec(memory_space=VMEM)],
        out_specs=pl.BlockSpec(memory_space=VMEM),
        scratch_shapes=[
            VMEM((devices - 1, share, BINS), jnp.float32),
            pltpu.SemaphoreType.DMA((devices - 1,)),
            pltpu.SemaphoreType.DMA((devices - 1,)),
        ],
        compiler_params=pltpu.CompilerParams(collective_id=1, has_side_effects=True),
    )(signal.T.reshape(devices, share, BINS))
    return state_next, signal


def solution(mesh):
    in_specs = (
        P(None, "gx", "yz", None),
        P("gx", "yz", None),
        P(("gx", "yz")),
        P(None, ("gx", "yz")),
        P(None, ("gx", "yz")),
        P(),
        P(("gx", "yz"), None),
    )
    out_specs = (P(None, "gx", "yz", None), P(("gx", "yz"), None))
    sizes = (mesh.shape["gx"], mesh.shape["yz"])
    return jax.shard_map(
        functools.partial(per_device, sizes),
        mesh=mesh, in_specs=in_specs, out_specs=out_specs, check_vma=False,
    )
```

profile of v0, /device:TPU:0, one launch (start us, length us, event | category | flops | bytes accessed | tf_op | source)
XLA Modules:
  0.0 74.6 jit_solution(8275130274437876857)
XLA Ops:
  0.6 1.3 %dynamic-slice_bitcast_fusion.table_ref = f32[1,188]{1,0:T(1,128)} fusion(f32[8,1,188]{2,1,0:T(1,128)} %constant.64.clone, s32[]{:T(128)S(6)} %select_n.26), kind=kLoop, calls=%fused_computation.11 | loop fusion | bytes 1508 | tf_op jit(solution)/shard_map/jit(dynamic_index_in_dim)/squeeze | solution.py:454
  1.9 1.3 %fusion.2 = (f32[192]{0:T(256)S(1)}, s32[192]{0:T(256)}) fusion(s32[192]{0:T(256)} %param.11, s32[]{:T(128)S(6)} %mul.15, s32[]{:T(128)S(6)} %mul.12), kind=kLoop, calls=%fused_computation.10 | loop fusion | flops 6912 | bytes 2312 | tf_op jit(solution)/shard_map/convert_element_type | solution.py:496
  3.2 0.7 pad_maximum_fusion
  3.9 0.8 %copy.18 = f32[7,192]{0,1:T(8,128)} copy(f32[7,192]{1,0:T(8,128)S(1)} %pad_maximum_fusion) | data formatting | bytes 10752 | tf_op jit(solution)/shard_map/concatenate | solution.py:495
  4.6 33.5 %shard_map.104 = (f32[5,48,256]{2,1,0:T(8,128)}, f32[5,48,256]{2,1,0:T(8,128)}, f32[5,48,256]{2,1,0:T(8,128)}, f32[5,48,256]{2,1,0:T(8,128)}, f32[3,32,8,256]{3,...) custom-call(f32[1,188]{1,0:T(1,128)} %dynamic-slice_bitcast_fusion.table_ref, ...), custom_call_target="tpu_custom_call" | custom-call | tf_op jit(solution)/shard_map/pallas_call | solution.py:463
  38.2 23.1 %shard_map.105 = (f32[4,32,48,256]{3,2,1,0:T(8,128)}, f32[64,512]{1,0:T(8,128)}) custom-call(s32[1,192]{1,0:T(1,128)} %bitcast.11, f32[1,188]{1,0:T(1,128)} %dynamic-slice_bitcast_fusion.table_ref, f32[4,32,48,256]{3,2,1,0:T(8,128)} %state_ref.3, f32[32,48,256]{2,1,0:T(8,128)} %flow_ref.3, f32[5,48,256]{2,1,0:T(8,128)} %get-tuple-element.11.left_sum, ...), custom_call_target="tpu_custom_call" | custom-call | tf_op jit(solution)/shard_map/pallas_call | solution.py:503
  61.3 1.7 %copy.19 = f32[512,64]{1,0:T(8,128)} copy(f32[512,64]{0,1:T(8,128)} %bitcast.9) | data formatting | bytes 262144 | tf_op jit(solution)/shard_map/transpose | solution.py:549
  63.1 10.2 %shard_map.106 = f32[16,64]{1,0:T(8,128)} custom-call(f32[32,16,64]{2,1,0:T(8,128)} %bitcast.7), custom_call_target="tpu_custom_call" | custom-call | tf_op jit(solution)/shard_map/pallas_call | solution.py:538
  73.3 1.3 %copy.21 = f32[16,64]{1,0:T(8,128)} copy(f32[16,64]{1,0:T(8,128)} %shard_map.106) | data formatting | bytes 8192
where the time goes:
time: 75.5 us; the launch traced here: 74.6 us
  Pallas kernels  66.9 us (89%)
  local copies, waits for them, and re-layouts  5.04 us (7%)
  other arithmetic  1.99 us (3%)
    pallas_call x1, Pallas kernels, per_device(): pl.pallas_call(functools.partial(exchange_kernel, sizes), out_shape=(plan...  33.5 us
    pallas_call x1, Pallas kernels, per_device(): pl.pallas_call(functools.partial(main_kernel, cells, width, depth), grid=...  23.1 us
    pallas_call x1, Pallas kernels, per_device(): pl.pallas_call(functools.partial(signal_kernel, groups, devices), out_sha...  10.2 us
    transpose x1, local copies, waits for them, and re-layouts, per_device(): signal.T.reshape(devices, share, BINS)  1.72 us

commit v1 on v0

v1 whole, which is shorter than its diff:
```python
import functools

import numpy as np
import jax
import jax.numpy as jnp
from jax import lax
from jax.experimental import pallas as pl
from jax.experimental.pallas import tpu as pltpu
from jax.sharding import PartitionSpec as P

BINS = 64
TILE = 8
LANES = 128
REACH = 3
VMEM_MIB = 54

time_step = 0.25
four_pi = 4.0 * 3.141592653589793
VMEM = pltpu.VMEM
SMEM = pltpu.SMEM
HBM = pltpu.HBM
MESH = pl.DeviceIdType.MESH

PADDED = (0, 2, 4)
PLAIN = (1, 3)


def diagonals(count):
    lower = np.full(count, 1.0 / 3.0)
    upper = np.full(count, 1.0 / 3.0)
    lower[1] = lower[count - 2] = upper[1] = upper[count - 2] = 0.25
    lower[0] = upper[count - 1] = 0.0
    lower[count - 1] = upper[0] = 2.0
    return lower, upper


def stencil(count):
    rows = np.zeros((count, count))
    for i in range(2, count - 2):
        rows[i, i + 1], rows[i, i - 1] = 7.0 / 9.0, -7.0 / 9.0
        rows[i, i + 2], rows[i, i - 2] = 1.0 / 36.0, -1.0 / 36.0
    rows[0, :3] = (-2.5, 2.0, 0.5)
    rows[1, 0], rows[1, 2] = -0.75, 0.75
    rows[count - 2, count - 3], rows[count - 2, count - 1] = -0.75, 0.75
    rows[count - 1, count - 3:] = (-0.5, -2.0, 2.5)
    return rows


def dense_derivative(count):
    lower, upper = diagonals(count)
    matrix = np.eye(count) + np.diag(lower[1:], -1) + np.diag(upper[:-1], 1)
    return np.linalg.solve(matrix, stencil(count))


class Table:
    def __init__(self, blocks, cells):
        count = blocks * cells
        lower, upper = diagonals(count)
        rows = stencil(count)
        down, pivot = np.zeros(count), np.ones(count)
        for i in range(1, count):
            down[i] = lower[i] / pivot[i - 1]
            pivot[i] = 1.0 - down[i] * upper[i - 1]
        up, pivot_up = np.zeros(count), np.ones(count)
        for i in range(count - 2, -1, -1):
            up[i] = upper[i] / pivot_up[i + 1]
            pivot_up[i] = 1.0 - up[i] * lower[i + 1]
        from_left = rows.copy()
        for i in range(1, count):
            from_left[i] -= down[i] * from_left[i - 1]
        from_right = rows.copy()
        for i in range(count - 2, -1, -1):
            from_right[i] -= up[i] * from_right[i + 1]
        part = {
            "right": np.zeros((blocks, cells)), "left": np.zeros((blocks, cells)),
            "near": np.zeros((blocks, cells)), "wide": np.zeros((blocks, cells)),
            "back": np.zeros((blocks, cells)), "ahead": np.zeros((blocks, cells)),
            "edge": np.zeros((blocks, 4, 4)), "link": np.zeros((blocks, 4)),
            "ends": np.zeros((blocks, 4)),
        }
        chain = np.zeros((blocks, 2))
        for d in range(blocks):
            s, e = d * cells, (d + 1) * cells
            if d < blocks - 1:
                part["right"][d] = from_left[e + 1, s:e]
                chain[d, 0] = np.prod(-down[s + 2:e + 2])
            if d > 0:
                part["left"][d] = from_right[s - 2, s:e]
                chain[d, 1] = np.prod(-up[s - 2:e - 2])
            inverse = 1.0 / pivot[s:e]
            inverse[-1] = 1.0 / (pivot[e - 1] + pivot_up[e - 1] - 1.0)
            part["near"][d] = 7.0 / 9.0 * inverse
            part["wide"][d] = 1.0 / 36.0 * inverse
            part["back"][d] = lower[s:e] * inverse
            part["ahead"][d] = upper[s:e] / pivot[s:e]
            part["edge"][d, 0, :3] = from_left[s, s:s + 3] * inverse[0]
            part["edge"][d, 1] = rows[s + 1, s:s + 4] * inverse[1]
            part["edge"][d, 2] = rows[e - 2, e - 4:e] * inverse[-2]
            part["edge"][d, 3, 1:] = from_right[e - 1, e - 3:e] * inverse[-1]
            part["ends"][d, 0] = -inverse[0] / down[s + 1]
            part["ends"][d, 1] = -inverse[-1] / up[e - 2]
            if d > 0:
                part["ends"][d, 2] = rows[s + 1, s - 1] / lower[s + 1]
            if d < blocks - 1:
                part["ends"][d, 3] = rows[e - 2, e] / upper[e - 2]
        part["link"][1:, 0] = chain[1:, 0] * chain[:-1, 0]
        part["link"][:-1, 1] = chain[:-1, 1] * chain[1:, 1]
        part["link"][1:, 2] = chain[:-1, 0]
        part["link"][:-1, 3] = chain[1:, 1]
        largest, hops, reach = np.abs(chain).max(), 1, np.abs(chain).max()
        while hops < blocks - 1 and reach >= np.finfo(np.float32).tiny:
            hops, reach = hops + 1, reach * largest
        assert hops <= 3
        self.at, column = {}, 0
        for name, values in part.items():
            self.at[name] = column
            column += values[0].size
        self.stride = column
        self.values = np.concatenate(
            [values.reshape(blocks, -1) for values in part.values()], axis=1
        ).astype(np.float32).reshape(-1)


def quotient(largest, divisor):
    for shift in range(31):
        factor = -(-(1 << shift) // divisor)
        excess = factor * divisor - (1 << shift)
        if excess * (largest - 1) < (1 << shift) and factor * (largest - 1) < 2**31:
            return factor, shift
    raise AssertionError("no factor")


def fused_kernel(
    sizes, where, stride,
    table_ref, cell_ref, state_ref, flow_ref, zhi_in, zlo_in,
    cells_ref, normal_ref, pos_ref, observer_ref, bin_in,
    next_ref, signal_ref,
    zhi_ref, zlo_ref, bin_ref, pad, plain, base, swept, rate,
    to_right, to_left, left_sum, right_sum, on_right, on_left, far_left, far_right,
    left_plane, right_plane,
    geometry, kernels, picked, contribution, binned, pieces, landing,
    load_sem, halo_send, halo_recv, plane_send, plane_recv, sum_send, sum_recv,
    piece_send, piece_recv,
):
    blocks, groups = sizes
    _, cells, width, depth = next_ref.shape
    faces, observers = bin_ref.shape
    tiles, halves, count = width // TILE, depth // LANES, blocks * groups
    block, group = lax.axis_index("gx"), lax.axis_index("yz")
    me = block * groups + group
    row0 = block * stride

    def scalar(name, i=0):
        return table_ref[row0 + (where[name] + i)]

    place = {"gx": (block, blocks), "yz": (group, groups)}

    def there(axis, shift):
        index, number = place[axis]
        return index + shift < number if shift > 0 else index + shift >= 0

    def other(axis, shift):
        index, number = place[axis]
        return {axis: jnp.clip(index + shift, 0, number - 1)}

    def partner(k):
        index = lax.rem(me + k, count)
        return {"gx": lax.div(index, groups), "yz": lax.rem(index, groups)}, index

    barrier = pltpu.get_barrier_semaphore()
    for k in range(1, count):
        pl.semaphore_signal(barrier, inc=1, device_id=partner(k)[0], device_id_type=MESH)

    loads = []
    for slot, f in enumerate(PADDED):
        source = flow_ref if f == 4 else state_ref.at[f]
        for h in range(halves):
            loads.append(pltpu.make_async_copy(
                source.at[:, :, h * LANES:(h + 1) * LANES],
                pad.at[slot, h, :, TILE:TILE + width, :], load_sem.at[len(loads)],
            ))
    for slot, f in enumerate(PLAIN):
        loads.append(pltpu.make_async_copy(state_ref.at[f], plain.at[slot], load_sem.at[len(loads)]))
    spare = [
        pltpu.make_async_copy(source, target, load_sem.at[len(loads) + k])
        for k, (source, target) in enumerate(((zhi_in, zhi_ref), (zlo_in, zlo_ref), (bin_in, bin_ref)))
    ]
    for load in loads + spare:
        load.start()

    for axis, shift, targets in (
        ("gx", -1, (left_sum, left_plane)), ("gx", 1, (right_sum, right_plane)),
        ("gx", -2, (far_left,)), ("gx", 2, (far_right,)),
    ):
        @pl.when(jnp.logical_not(there(axis, shift)))
        def _():
            for target in targets:
                target[...] = jnp.zeros_like(target)
    for shift, at in ((-1, TILE - REACH), (1, TILE + width)):
        @pl.when(jnp.logical_not(there("yz", shift)))
        def _():
            pad[:, :, :, at:at + REACH, :] = jnp.zeros((len(PADDED), halves, cells, REACH, LANES), jnp.float32)

    def remote(source, target, send, recv, axis, shift):
        return pltpu.make_async_remote_copy(
            src_ref=source, dst_ref=target, send_sem=send, recv_sem=recv,
            device_id=other(axis, shift), device_id_type=MESH,
        )

    def start(copy, axis, shift):
        @pl.when(there(axis, shift))
        def _():
            copy.start()

    def arrive(copy, axis, shift):
        @pl.when(there(axis, -shift))
        def _():
            copy.wait_recv()

    def sent(copy, axis, shift):
        @pl.when(there(axis, shift))
        def _():
            copy.wait_send()

    def near(side, t):
        if side == 0:
            return remote(on_right.at[t], left_sum.at[t], sum_send.at[0, t], sum_recv.at[0, t], "gx", 1), "gx", 1
        return remote(on_left.at[t], right_sum.at[t], sum_send.at[1, t], sum_recv.at[1, t], "gx", -1), "gx", -1

    def far(side, t):
        if side == 0:
            return remote(to_right.at[t], far_left.at[t], sum_send.at[2, t], sum_recv.at[2, t], "gx", 2), "gx", 2
        return remote(to_left.at[t], far_right.at[t], sum_send.at[3, t], sum_recv.at[3, t], "gx", -2), "gx", -2

    halos = [
        (remote(pad.at[:, :, :, TILE + width - REACH:TILE + width, :], pad.at[:, :, :, TILE - REACH:TILE, :],
                halo_send.at[0], halo_recv.at[0], "yz", 1), "yz", 1),
        (remote(pad.at[:, :, :, TILE:TILE + REACH, :], pad.at[:, :, :, TILE + width:TILE + width + REACH, :],
                halo_send.at[1], halo_recv.at[1], "yz", -1), "yz", -1),
    ]
    planes = [[], []]
    for side, (at, target, shift) in enumerate(((cells - 1, left_plane, 1), (0, right_plane, -1))):
        for piece, (source, into) in enumerate((
            (state_ref.at[0:2, at], target.at[0:2]), (state_ref.at[2:4, at], target.at[2:4]),
            (flow_ref.at[at], target.at[4]),
        )):
            planes[min(piece, 1)].append((remote(
                source, into, plane_send.at[side, piece], plane_recv.at[side, piece], "gx", shift
            ), "gx", shift))

    def value(f, i, rows, h):
        if f in PADDED:
            return pad[PADDED.index(f), h, i, pl.ds(rows + TILE, TILE), :]
        return plain[PLAIN.index(f), i, pl.ds(rows, TILE), h * LANES:(h + 1) * LANES]

    def first_row(t):
        return pl.multiple_of(t * TILE, TILE)

    pl.semaphore_wait(barrier, count - 1)
    for entry in planes[0]:
        start(*entry)
    for load in loads[:len(PADDED) * halves]:
        load.wait()
    for entry in halos:
        start(*entry)
    for load in loads[len(PADDED) * halves:] + spare:
        load.wait()

    fields = range(5)
    pairs = [(f, h) for f in fields for h in range(halves)]

    def sums(t, carry):
        rows = first_row(t)
        totals = None
        for i in range(cells):
            weights = scalar("right", i), scalar("left", i)
            now = [value(f, i, rows, h) for f, h in pairs]
            terms = [[weight * one for weight in weights] for one in now]
            totals = terms if totals is None else [
                [old + new for old, new in zip(*both)] for both in zip(totals, terms)
            ]
        for (f, h), (total_right, total_left) in zip(pairs, totals):
            lanes = slice(h * LANES, (h + 1) * LANES)
            to_right[t, f, :, lanes] = total_right
            to_left[t, f, :, lanes] = total_left
        start(*far(0, t))
        start(*far(1, t))
        return carry

    lax.fori_loop(0, tiles, sums, 0)

    together = 4 if cells % 4 == 0 else 1

    def multiply(k, carry):
        span = pl.ds(k * together, together)
        for f, target in ((0, 3), (3, 0), (4, 1)):
            if f in PADDED:
                lines = jnp.concatenate([
                    pad[PADDED.index(f), h, span, TILE:TILE + width, :].reshape(together * width, LANES)
                    for h in range(halves)
                ], axis=1)
            else:
                lines = plain[PLAIN.index(f), span].reshape(together * width, depth)
            high = lines.astype(jnp.bfloat16)
            rest = (lines - high.astype(jnp.float32)).astype(jnp.bfloat16)
            out = jnp.dot(rest, zhi_ref[...], preferred_element_type=jnp.float32)
            out += jnp.dot(high, zlo_ref[...], preferred_element_type=jnp.float32)
            out += jnp.dot(high, zhi_ref[...], preferred_element_type=jnp.float32)
            base[target, span] = out.reshape(together, width, depth)
        return carry

    lax.fori_loop(0, cells // together, multiply, 0)

    geometry[...] = jnp.zeros_like(geometry)
    geometry[0:3, 0:faces] = normal_ref[...]
    geometry[3:6, 0:faces] = pos_ref[...]
    along_z = cells_ref[...] & (depth - 1) if depth & (depth - 1) == 0 else lax.rem(cells_ref[...], depth)
    geometry[6:7, 0:faces] = along_z.astype(jnp.float32)
    columns = geometry[...].T

    def column(c):
        return columns[0:faces, c:c + 1]

    normal = [column(c) for c in range(3)]
    offset = [observer_ref[c:c + 1, :] - column(3 + c) for c in range(3)]
    distance = jnp.sqrt(offset[0] * offset[0] + offset[1] * offset[1] + offset[2] * offset[2])
    normal_r = (normal[0] * offset[0] + normal[1] * offset[1] + normal[2] * offset[2]) / distance
    scale = 1.0 / (four_pi * distance)
    kernels[0] = scale
    kernels[1] = normal_r * scale
    kernels[2] = normal_r * scale / distance

    def relay(t):
        arrive(*far(0, t))
        arrive(*far(1, t))
        on_right[t] = to_right[t] + scalar("link", 0) * far_left[t]
        on_left[t] = to_left[t] + scalar("link", 1) * far_right[t]
        start(*near(0, t))
        start(*near(1, t))

    for entry in halos:
        arrive(*entry)

    def lateral(i, carry):
        for t in range(tiles):
            rows = t * TILE
            for h in range(halves):
                lanes = slice(h * LANES, (h + 1) * LANES)

                def y_rate(slot):
                    def take(shift):
                        return pad[slot, h, i, TILE + rows + shift:2 * TILE + rows + shift, :]
                    return (
                        0.75 * (take(1) - take(-1)) - 0.15 * (take(2) - take(-2))
                        + 1.0 / 60.0 * (take(3) - take(-3))
                    )

                spot = (i, slice(rows, rows + TILE), lanes)
                base[(0,) + spot] = base[(0,) + spot] + y_rate(1)
                base[(1,) + spot] = value(2, i, rows, h) * y_rate(2) + value(3, i, rows, h) * base[(1,) + spot]
                base[(2,) + spot] = y_rate(0)
        return carry

    pumps = min(tiles, cells)
    for t in range(pumps):
        relay(t)
        lax.fori_loop(cells * t // pumps, cells * (t + 1) // pumps, lateral, 0)
    for entry in planes[1]:
        start(*entry)

    chunk = 4
    assert cells % chunk == 0 and cells >= 3 * chunk

    def finish(t):
        arrive(*near(0, t))
        arrive(*near(1, t))
        rows = first_row(t)
        n = cells
        carry = []
        edge = [scalar("edge", j) for j in range(8)]
        link, end, back = scalar("link", 2), scalar("ends", 0), scalar("back", 1)
        for f, h in pairs:
            lanes = slice(h * LANES, (h + 1) * LANES)
            own = [value(f, i, rows, h) for i in range(4)]
            incoming = left_sum[t, f, :, lanes] + link * far_left[t, f, :, lanes]
            first = edge[0] * own[0] + edge[1] * own[1] + edge[2] * own[2] + end * incoming
            second = edge[4] * own[0] + edge[5] * own[1] + edge[6] * own[2] + edge[7] * own[3] - back * first
            swept[f, 0, :, lanes] = first
            swept[f, 1, :, lanes] = second
            carry.append(second)

        def forward(k, carry):
            i0 = 2 + k * chunk
            new = list(carry)
            factors = [[scalar(name, i0 + j) for name in ("near", "wide", "back")] for j in range(chunk)]
            for p, (f, h) in enumerate(pairs):
                lanes = slice(h * LANES, (h + 1) * LANES)
                own = [value(f, i0 + j, rows, h) for j in range(-2, chunk + 2)]
                for j in range(chunk):
                    close, wide, back = factors[j]
                    new[p] = close * (own[j + 3] - own[j + 1]) + wide * (own[j + 4] - own[j]) - back * new[p]
                    swept[f, i0 + j, :, lanes] = new[p]
            return tuple(new)

        carry = lax.fori_loop(0, (n - 4) // chunk, forward, tuple(carry))
        solved = []
        edge = [scalar("edge", 8 + j) for j in range(8)]
        link, end, back, last = scalar("link", 3), scalar("ends", 1), scalar("back", n - 2), scalar("back", n - 1)
        for p, (f, h) in enumerate(pairs):
            lanes = slice(h * LANES, (h + 1) * LANES)
            own = [value(f, i, rows, h) for i in range(n - 4, n)]
            incoming = right_sum[t, f, :, lanes] + link * far_right[t, f, :, lanes]
            before = (
                edge[0] * own[0] + edge[1] * own[1] + edge[2] * own[2] + edge[3] * own[3] - back * carry[p]
            )
            swept[f, n - 2, :, lanes] = before
            solved.append(
                edge[5] * own[1] + edge[6] * own[2] + edge[7] * own[3] + end * incoming - last * before
            )

        def store(i, x):
            spot = pl.ds(pl.multiple_of(i * width + rows, TILE), TILE)
            for h in range(halves):
                lanes = slice(h * LANES, (h + 1) * LANES)
                old = [value(f, i, rows, h) for f in fields]
                flow = old[4]
                px, ux, vx, wx, fx = (x[f * halves + h] for f in fields)
                terms = [base[c, i, pl.ds(rows, TILE), lanes] for c in range(4)]
                losses = (
                    flow * px + ux + terms[0],
                    flow * ux + old[1] * fx + px + terms[1],
                    flow * vx + terms[2],
                    flow * wx + terms[3],
                )
                for c in range(4):
                    rate[c, spot, lanes] = losses[c]
                    next_ref[c, i, pl.ds(rows, TILE), lanes] = old[c] - time_step * losses[c]

        def step_back(i, x):
            ahead = scalar("ahead", i)
            x = [
                swept[f, i, :, h * LANES:(h + 1) * LANES] - ahead * x[p]
                for p, (f, h) in enumerate(pairs)
            ]
            store(i, x)
            return x

        store(n - 1, solved)
        for j in range(2, chunk + 1):
            solved = step_back(n - j, solved)

        def backward(k, x):
            for j in range(chunk):
                x = step_back(n - chunk - 1 - k * chunk - j, x)
            return tuple(x)

        lax.fori_loop(0, n // chunk - 1, backward, tuple(solved))

    def main(t, carry):
        finish(t)
        return carry

    lax.fori_loop(0, tiles, main, 0)

    for entry in planes[0] + planes[1]:
        arrive(*entry)

    def mend(t, carry):
        rows = first_row(t)
        for at, plane, end in ((0, left_plane, 2), (cells - 1, right_plane, 3)):
            spot = pl.ds(pl.multiple_of(at * width + rows, TILE), TILE)
            for h in range(halves):
                lanes = slice(h * LANES, (h + 1) * LANES)
                px, ux, vx, wx, fx = (scalar("ends", end) * plane[f, pl.ds(rows, TILE), lanes] for f in fields)
                stream, flow = value(1, at, rows, h), value(4, at, rows, h)
                more = (flow * px + ux, flow * ux + stream * fx + px, flow * vx, flow * wx)
                for c in range(4):
                    rate[c, spot, lanes] = rate[c, spot, lanes] + more[c]
                    next_ref[c, at, pl.ds(rows, TILE), lanes] = (
                        next_ref[c, at, pl.ds(rows, TILE), lanes] - time_step * more[c]
                    )
        return carry

    lax.fori_loop(0, tiles, mend, 0)

    factor, shift = quotient(cells * width * groups, width * groups)
    power = depth.bit_length() - 1
    origin = block * (cells * width * groups)

    def pick(k, carry):
        cell = cell_ref[k]
        line = (cell >> power if depth & (depth - 1) == 0 else lax.div(cell, depth)) - origin
        along_x = (line * factor) >> shift
        along_y = jnp.clip(line - along_x * (width * groups) - group * width, 0, width - 1)
        along_x = jnp.clip(along_x, 0, cells - 1)
        row = along_x * width + along_y
        for c in range(4):
            picked[c, pl.ds(k, 1), :] = rate[c, pl.ds(row, 1), :]
        picked[4, pl.ds(k, 1), :] = next_ref[0, along_x, pl.ds(along_y, 1), :]
        return carry

    lax.fori_loop(0, faces, pick, 0, unroll=4)
    mask = lax.broadcasted_iota(jnp.int32, (faces, depth), 1) == column(6).astype(jnp.int32)
    at = [jnp.sum(jnp.where(mask, picked[c], 0.0), axis=1, keepdims=True) for c in range(5)]
    normal_rate = normal[0] * at[1] + normal[1] * at[2] + normal[2] * at[3]
    contribution[...] = at[4] * kernels[2] - at[0] * kernels[1] - normal_rate * kernels[0]

    def gather(b, carry):
        binned[pl.ds(b, 1), :] = jnp.sum(
            jnp.where(bin_ref[...] == b, contribution[...], 0.0), axis=0, keepdims=True
        )
        return carry

    lax.fori_loop(0, BINS, gather, 0, unroll=2)
    share, beside = observers // count, LANES // BINS
    dense = share % (TILE * beside) == 0
    if not dense:
        pieces[...] = jnp.zeros_like(pieces)
    turned = jnp.concatenate([binned[...], jnp.zeros((LANES - BINS, observers), jnp.float32)], axis=0).T
    if dense:
        turned = turned.reshape(count, share // TILE, TILE, LANES)
        lane = lax.broadcasted_iota(jnp.int32, (count * TILE, LANES), 1)
        for q in range(share // TILE // beside):
            row = turned[:, q * beside].reshape(count * TILE, LANES)
            for j in range(1, beside):
                moved = pltpu.roll(turned[:, q * beside + j].reshape(count * TILE, LANES), j * BINS, 1)
                row = jnp.where(lane >= j * BINS, moved, row)
            pieces[:, q] = row.reshape(count, TILE, LANES)
    else:
        for d in range(count):
            pieces[d, 0, 0:share, :] = turned[d * share:(d + 1) * share]
    copies = []
    for k in range(1, count):
        target, index = partner(k)
        copies.append(pltpu.make_async_remote_copy(
            src_ref=pieces.at[index], dst_ref=landing.at[k - 1],
            send_sem=piece_send.at[k - 1], recv_sem=piece_recv.at[k - 1],
            device_id=target, device_id_type=MESH,
        ))
        copies[-1].start()
    total = pieces[me]
    for k in range(count - 1):
        copies[k].wait_recv()
        total += landing[k]
    if dense:
        for q in range(share // TILE // beside):
            for j in range(beside):
                moved = total[q] if j == 0 else pltpu.roll(total[q], LANES - j * BINS, 1)
                top = (q * beside + j) * TILE
                signal_ref[top:top + TILE, :] = moved[:, 0:BINS]
    else:
        signal_ref[...] = total[0, 0:share, 0:BINS]

    for k in range(count - 1):
        copies[k].wait_send()
    for entry in halos + planes[0] + planes[1]:
        sent(*entry)

    def drain(t, carry):
        for side in (0, 1):
            sent(*near(side, t))
            sent(*far(side, t))
        return carry

    lax.fori_loop(0, tiles, drain, 0)


def copy_kernel(next_ref, signal_ref, next_out, signal_out, sems):
    copies = [
        pltpu.make_async_copy(next_ref, next_out, sems.at[0]),
        pltpu.make_async_copy(signal_ref, signal_out, sems.at[1]),
    ]
    for copy in copies:
        copy.start()
    for copy in copies:
        copy.wait()


def per_device(sizes, state, mean_flow, face_cell, face_normal, face_pos, observer_pos, time_bin):
    blocks, groups = sizes
    _, cells, width, depth = state.shape
    faces, observers = time_bin.shape
    tiles, halves, devices = width // TILE, depth // LANES, blocks * groups
    share = observers // devices
    dense = share % (TILE * (LANES // BINS)) == 0
    packed = (share * BINS // (TILE * LANES), TILE, LANES) if dense else (1, -(-share // TILE) * TILE, LANES)
    table = Table(blocks, cells)
    operator = dense_derivative(depth).T.astype(np.float32)
    z_high = jnp.asarray(operator).astype(jnp.bfloat16)
    z_low = (jnp.asarray(operator) - z_high.astype(jnp.float32)).astype(jnp.bfloat16)
    f32 = jnp.float32
    padded_faces = -(-faces // LANES) * LANES
    smem, vmem, hbm = (pl.BlockSpec(memory_space=space) for space in (SMEM, VMEM, HBM))
    dma = pltpu.SemaphoreType.DMA
    sums = VMEM((tiles, 5, TILE, depth), f32)
    state_next, signal = pl.pallas_call(
        functools.partial(fused_kernel, sizes, table.at, table.stride),
        out_shape=(VMEM(state.shape, f32), VMEM((share, BINS), f32)),
        in_specs=[smem, smem, hbm, hbm, hbm, hbm, vmem, vmem, vmem, vmem, hbm],
        out_specs=(vmem, vmem),
        scratch_shapes=[
            VMEM((depth, depth), jnp.bfloat16), VMEM((depth, depth), jnp.bfloat16),
            VMEM((faces, observers), jnp.int32),
            VMEM((len(PADDED), halves, cells, width + 2 * TILE, LANES), f32),
            VMEM((len(PLAIN), cells, width, depth), f32),
            VMEM((4, cells, width, depth), f32),
            VMEM((5, cells, TILE, depth), f32),
            VMEM((4, cells * width, depth), f32),
        ] + [sums] * 8 + [
            VMEM((5, width, depth), f32), VMEM((5, width, depth), f32),
            VMEM((TILE, padded_faces), f32), VMEM((3, faces, observers), f32),
            VMEM((5, faces, depth), f32), VMEM((faces, observers), f32),
            VMEM((BINS, observers), f32), VMEM((devices,) + packed, f32),
            VMEM((devices - 1,) + packed, f32),
            dma((len(PADDED) * halves + len(PLAIN) + 3,)), dma((2,)), dma((2,)), dma((2, 3)), dma((2, 3)),
            dma((4, tiles)), dma((4, tiles)), dma((devices - 1,)), dma((devices - 1,)),
        ],
        compiler_params=pltpu.CompilerParams(
            collective_id=0, has_side_effects=True, vmem_limit_bytes=VMEM_MIB * 1024 * 1024
        ),
    )(
        jnp.asarray(table.values), face_cell, state, mean_flow, z_high, z_low,
        face_cell.reshape(1, faces), face_normal, face_pos, observer_pos, time_bin,
    )
    return pl.pallas_call(
        copy_kernel,
        out_shape=(
            jax.ShapeDtypeStruct(state.shape, f32),
            jax.ShapeDtypeStruct((share, BINS), f32),
        ),
        in_specs=[vmem, vmem],
        out_specs=(hbm, hbm),
        scratch_shapes=[dma((2,))],
        compiler_params=pltpu.CompilerParams(vmem_limit_bytes=8 * 1024 * 1024),
    )(state_next, signal)


def solution(mesh):
    in_specs = (
        P(None, "gx", "yz", None),
        P("gx", "yz", None),
        P(("gx", "yz")),
        P(None, ("gx", "yz")),
        P(None, ("gx", "yz")),
        P(),
        P(("gx", "yz"), None),
    )
    out_specs = (P(None, "gx", "yz", None), P(("gx", "yz"), None))
    sizes = (mesh.shape["gx"], mesh.shape["yz"])
    return jax.shard_map(
        functools.partial(per_device, sizes),
        mesh=mesh, in_specs=in_specs, out_specs=out_specs, check_vma=False,
    )
```

time: 75.5 us -> 49.1 us (0.65)
  Pallas kernels: 66.9 us -> 48.3 us
  local copies, waits for them, and re-layouts: 5.04 us -> 0 us
  other arithmetic: 1.99 us -> 0 us
    pallas_call x3 -> x2, Pallas kernels: 66.9 us -> 48.3 us  [the longest x1 45.5 us: per_device(): pl.pallas_call(functools.partial(fused_kernel, sizes, table.at, table.str...]
    transpose x1 -> x0, local copies, waits for them, and re-layouts: 1.72 us -> none  [per_device(): signal.T.reshape(devices, share, BINS)]
    unnamed x1 -> x0, local copies, waits for them, and re-layouts: 1.3 us -> none
    convert_element_type x1 -> x0, other arithmetic: 1.26 us -> none  [per_device(): along_z.astype(jnp.float32)[None]]
    squeeze x1 -> x0, local copies, waits for them, and re-layouts: 1.26 us -> none  [per_device(): lax.dynamic_index_in_dim(jnp.asarray(tables), block, 0, keepdims=False)]
    concatenate x1 -> x0, local copies, waits for them, and re-layouts: 0.76 us -> none  [per_device(): jnp.concatenate([face_normal, face_pos, along_z.astype(jnp.float32)[None]])]
where the time goes in v1:
time: 49.1 us; the launch traced here: 48.9 us
  Pallas kernels  48.3 us (98%)
  between operations  0.64 us (1%)
    pallas_call x1, Pallas kernels, per_device(): pl.pallas_call(functools.partial(fused_kernel, sizes, table.at, table.str...  45.5 us
    pallas_call x1, Pallas kernels, per_device(): pl.pallas_call(copy_kernel, out_shape=(jax.ShapeDtypeStruct(state.shape,...  2.72 us

profile of v1, /device:TPU:0, one launch (start us, length us, event | category | flops | bytes accessed | tf_op | source)
XLA Modules:
  0.0 48.9 jit_solution(12022943390502600168)
XLA Ops:
  0.6 45.5 %shard_map.104 = (f32[4,32,48,256]{3,2,1,0:T(8,128)S(1)}, f32[16,64]{1,0:T(8,128)S(1)}) custom-call(f32[1728]{0:T(1024)} %constant.5.clone.table_ref, s32[192]{0:T(256)} %cell_ref.1, f32[4,32,48,256]{3,2,1,0:T(8,128)} %state_ref.1, f32[32,48,256]{2,1,0:T(8,128)} %flow_ref.1, bf16[256,256]{1,0:T(8,128)(2,1)} %constant.6.zhi_in, ...), custom_call_target="tpu_custom_call" | custom-call | tf_op jit(solution)/shard_map/pallas_call | solution.py:596
  46.2 2.7 %shard_map.105 = (f32[4,32,48,256]{3,2,1,0:T(8,128)}, f32[16,64]{1,0:T(8,128)}) custom-call(f32[4,32,48,256]{3,2,1,0:T(8,128)S(1)} %get-tuple-element.4.next_ref, f32[16,64]{1,0:T(8,128)S(1)} %get-tuple-element.5.signal_ref), custom_call_target="tpu_custom_call" | custom-call | tf_op jit(solution)/shard_map/pallas_call | solution.py:625

commit v2 on v1

--- a/solution.py
+++ b/solution.py
@@ -13,6 +13,7 @@
 LANES = 128
 REACH = 3
 VMEM_MIB = 54
+EARLY = ()
 
 time_step = 0.25
 four_pi = 4.0 * 3.141592653589793
@@ -139,8 +140,9 @@
     to_right, to_left, left_sum, right_sum, on_right, on_left, far_left, far_right,
     left_plane, right_plane,
     geometry, kernels, picked, contribution, binned, pieces, landing,
+    lines, chosen, ask, asked, reply, got, mends, columns_ref, own_ref,
     load_sem, halo_send, halo_recv, plane_send, plane_recv, sum_send, sum_recv,
-    piece_send, piece_recv,
+    piece_send, piece_recv, ask_send, ask_recv, reply_send, reply_recv,
 ):
     blocks, groups = sizes
     _, cells, width, depth = next_ref.shape
@@ -166,10 +168,6 @@
     def partner(k):
         index = lax.rem(me + k, count)
         return {"gx": lax.div(index, groups), "yz": lax.rem(index, groups)}, index
-
-    barrier = pltpu.get_barrier_semaphore()
-    for k in range(1, count):
-        pl.semaphore_signal(barrier, inc=1, device_id=partner(k)[0], device_id_type=MESH)
 
     loads = []
     for slot, f in enumerate(PADDED):
@@ -188,8 +186,13 @@
     for load in loads + spare:
         load.start()
 
+    barrier = pltpu.get_barrier_semaphore()
+    for k in range(1, count):
+        pl.semaphore_signal(barrier, inc=1, device_id=partner(k)[0], device_id_type=MESH)
+
     for axis, shift, targets in (
-        ("gx", -1, (left_sum, left_plane)), ("gx", 1, (right_sum, right_plane)),
+        ("gx", -1, (left_sum, left_plane, asked.at[0], got.at[0])),
+        ("gx", 1, (right_sum, right_plane, asked.at[1], got.at[1])),
         ("gx", -2, (far_left,)), ("gx", 2, (far_right,)),
     ):
         @pl.when(jnp.logical_not(there(axis, shift)))
@@ -244,7 +247,7 @@
             (state_ref.at[0:2, at], target.at[0:2]), (state_ref.at[2:4, at], target.at[2:4]),
             (flow_ref.at[at], target.at[4]),
         )):
-            planes[min(piece, 1)].append((remote(
+            planes[0 if piece in EARLY else 1].append((remote(
                 source, into, plane_send.at[side, piece], plane_recv.at[side, piece], "gx", shift
             ), "gx", shift))
 
@@ -256,7 +259,32 @@
     def first_row(t):
         return pl.multiple_of(t * TILE, TILE)
 
+    factor, shift = quotient(cells * width * groups, width * groups)
+    power = depth.bit_length() - 1
+    origin = block * (cells * width * groups)
+
+    def locate(cell):
+        line = (cell >> power if depth & (depth - 1) == 0 else lax.div(cell, depth)) - origin
+        along_x = (line * factor) >> shift
+        return along_x, line - along_x * (width * groups) - group * width
+
+    ask[...] = jnp.full_like(ask, -1.0)
+    along_x, along_y = locate(cells_ref[...])
+    along_z = cells_ref[...] & (depth - 1) if depth & (depth - 1) == 0 else lax.rem(cells_ref[...], depth)
+    for k, along in enumerate((along_y, along_z, along_x)):
+        ask[k:k + 1, 0:faces] = along.astype(jnp.float32)
+    asks = [
+        (remote(ask, asked.at[0], ask_send.at[0], ask_recv.at[0], "gx", 1), "gx", 1),
+        (remote(ask, asked.at[1], ask_send.at[1], ask_recv.at[1], "gx", -1), "gx", -1),
+    ]
+    replies = [
+        (remote(reply.at[0], got.at[1], reply_send.at[0], reply_recv.at[0], "gx", -1), "gx", -1),
+        (remote(reply.at[1], got.at[0], reply_send.at[1], reply_recv.at[1], "gx", 1), "gx", 1),
+    ]
+
     pl.semaphore_wait(barrier, count - 1)
+    for entry in asks:
+        start(*entry)
     for entry in planes[0]:
         start(*entry)
     for load in loads[:len(PADDED) * halves]:
@@ -289,6 +317,15 @@
 
     lax.fori_loop(0, tiles, sums, 0)
 
+    def relay(t):
+        arrive(*far(0, t))
+        arrive(*far(1, t))
+        on_right[t] = to_right[t] + scalar("link", 0) * far_left[t]
+        on_left[t] = to_left[t] + scalar("link", 1) * far_right[t]
+        start(*near(0, t))
+        start(*near(1, t))
+
+
     together = 4 if cells % 4 == 0 else 1
 
     def multiply(k, carry):
@@ -309,17 +346,88 @@
             base[target, span] = out.reshape(together, width, depth)
         return carry
 
-    lax.fori_loop(0, cells // together, multiply, 0)
+    steps = cells // together
+    lax.fori_loop(0, steps // 2, multiply, 0)
+    relay(0)
+    lax.fori_loop(steps // 2, steps, multiply, 0)
+
+    for entry in halos:
+        arrive(*entry)
+
+    def lateral(i, carry):
+        for t in range(tiles):
+            rows = t * TILE
+            for h in range(halves):
+                lanes = slice(h * LANES, (h + 1) * LANES)
+
+                def y_rate(slot):
+                    def take(shift):
+                        return pad[slot, h, i, TILE + rows + shift:2 * TILE + rows + shift, :]
+                    return (
+                        0.75 * (take(1) - take(-1)) - 0.15 * (take(2) - take(-2))
+                        + 1.0 / 60.0 * (take(3) - take(-3))
+                    )
+
+                spot = (i, slice(rows, rows + TILE), lanes)
+                base[(0,) + spot] = base[(0,) + spot] + y_rate(1)
+                base[(1,) + spot] = value(2, i, rows, h) * y_rate(2) + value(3, i, rows, h) * base[(1,) + spot]
+                base[(2,) + spot] = y_rate(0)
+        return carry
+
+    pumps = max(tiles - 1, 1)
+    for t in range(pumps):
+        if t + 1 < tiles:
+            relay(t + 1)
+        lax.fori_loop(cells * t // pumps, cells * (t + 1) // pumps, lateral, 0)
+
+    def plane_of(f, i):
+        if f in PADDED:
+            return jnp.concatenate(
+                [pad[PADDED.index(f), h, i, TILE:TILE + width, :] for h in range(halves)], axis=1
+            )
+        return plain[PLAIN.index(f), i]
+
+    def gather_columns(values, places):
+        ahead = lax.broadcasted_iota(jnp.int32, (depth, places.shape[1]), 0).astype(jnp.float32)
+        hot = jnp.where(ahead == places[1:2, :], 1.0, 0.0).astype(jnp.bfloat16)
+        rest, total = jnp.concatenate(values, axis=0), None
+        for _ in range(3):
+            part = rest.astype(jnp.bfloat16)
+            rest = rest - part.astype(jnp.float32)
+            product = jnp.dot(part, hot, preferred_element_type=jnp.float32)
+            total = product if total is None else total + product
+        here = lax.broadcasted_iota(jnp.int32, (width, places.shape[1]), 0).astype(jnp.float32) == places[0:1, :]
+        return [
+            jnp.sum(jnp.where(here, total[k * width:(k + 1) * width], 0.0), axis=0, keepdims=True)
+            for k in range(len(values))
+        ]
+
+    reply[...] = jnp.zeros_like(reply)
+    for side, at in ((0, 0), (1, cells - 1)):
+        arrive(*asks[side])
+        for k, row in enumerate(gather_columns([plane_of(f, at) for f in fields], asked[side])):
+            reply[side, k:k + 1, :] = row
+        start(*replies[side])
+    own = gather_columns([plane_of(f, at) for at in (0, cells - 1) for f in (1, 4)], ask[...])
+
+    def find(k, carry):
+        along_x, along_y = locate(cell_ref[k])
+        along_x, along_y = jnp.clip(along_x, 0, cells - 1), jnp.clip(along_y, 0, width - 1)
+        lines[k] = along_x * width + along_y
+        for h in range(halves):
+            chosen[h, pl.ds(k, 1), :] = pad[0, h, along_x, pl.ds(TILE + along_y, 1), :]
+        return carry
+
+    lax.fori_loop(0, faces, find, 0, unroll=4)
 
     geometry[...] = jnp.zeros_like(geometry)
     geometry[0:3, 0:faces] = normal_ref[...]
     geometry[3:6, 0:faces] = pos_ref[...]
-    along_z = cells_ref[...] & (depth - 1) if depth & (depth - 1) == 0 else lax.rem(cells_ref[...], depth)
     geometry[6:7, 0:faces] = along_z.astype(jnp.float32)
-    columns = geometry[...].T
+    columns_ref[...] = geometry[...].T
 
     def column(c):
-        return columns[0:faces, c:c + 1]
+        return columns_ref[0:faces, c:c + 1]
 
     normal = [column(c) for c in range(3)]
     offset = [observer_ref[c:c + 1, :] - column(3 + c) for c in range(3)]
@@ -329,51 +437,17 @@
     kernels[0] = scale
     kernels[1] = normal_r * scale
     kernels[2] = normal_r * scale / distance
-
-    def relay(t):
-        arrive(*far(0, t))
-        arrive(*far(1, t))
-        on_right[t] = to_right[t] + scalar("link", 0) * far_left[t]
-        on_left[t] = to_left[t] + scalar("link", 1) * far_right[t]
-        start(*near(0, t))
-        start(*near(1, t))
-
-    for entry in halos:
-        arrive(*entry)
-
-    def lateral(i, carry):
-        for t in range(tiles):
-            rows = t * TILE
-            for h in range(halves):
-                lanes = slice(h * LANES, (h + 1) * LANES)
-
-                def y_rate(slot):
-                    def take(shift):
-                        return pad[slot, h, i, TILE + rows + shift:2 * TILE + rows + shift, :]
-                    return (
-                        0.75 * (take(1) - take(-1)) - 0.15 * (take(2) - take(-2))
-                        + 1.0 / 60.0 * (take(3) - take(-3))
-                    )
-
-                spot = (i, slice(rows, rows + TILE), lanes)
-                base[(0,) + spot] = base[(0,) + spot] + y_rate(1)
-                base[(1,) + spot] = value(2, i, rows, h) * y_rate(2) + value(3, i, rows, h) * base[(1,) + spot]
-                base[(2,) + spot] = y_rate(0)
-        return carry
-
-    pumps = min(tiles, cells)
-    for t in range(pumps):
-        relay(t)
-        lax.fori_loop(cells * t // pumps, cells * (t + 1) // pumps, lateral, 0)
-    for entry in planes[1]:
-        start(*entry)
+    mask = lax.broadcasted_iota(jnp.int32, (faces, depth), 1) == column(6).astype(jnp.int32)
+    nearby = jnp.concatenate([chosen[h] for h in range(halves)], axis=1)
+    columns_ref[0:faces, 7:8] = jnp.sum(jnp.where(mask, nearby, 0.0), axis=1, keepdims=True)
+    own_ref[...] = jnp.zeros_like(own_ref)
+    for k, row in enumerate(own):
+        own_ref[k:k + 1, :] = row
 
     chunk = 4
     assert cells % chunk == 0 and cells >= 3 * chunk
 
     def finish(t):
-        arrive(*near(0, t))
-        arrive(*near(1, t))
         rows = first_row(t)
         n = cells
         carry = []
@@ -457,61 +531,66 @@
         lax.fori_loop(0, n // chunk - 1, backward, tuple(solved))
 
     def main(t, carry):
+        arrive(*near(0, t))
+        arrive(*near(1, t))
+
+        @pl.when(t == max(tiles - 2, 0))
+        def _():
+            for entry in planes[1]:
+                start(*entry)
+
         finish(t)
         return carry
 
     lax.fori_loop(0, tiles, main, 0)
 
-    for entry in planes[0] + planes[1]:
+    for entry in replies:
         arrive(*entry)
-
-    def mend(t, carry):
-        rows = first_row(t)
-        for at, plane, end in ((0, left_plane, 2), (cells - 1, right_plane, 3)):
-            spot = pl.ds(pl.multiple_of(at * width + rows, TILE), TILE)
-            for h in range(halves):
-                lanes = slice(h * LANES, (h + 1) * LANES)
-                px, ux, vx, wx, fx = (scalar("ends", end) * plane[f, pl.ds(rows, TILE), lanes] for f in fields)
-                stream, flow = value(1, at, rows, h), value(4, at, rows, h)
-                more = (flow * px + ux, flow * ux + stream * fx + px, flow * vx, flow * wx)
-                for c in range(4):
-                    rate[c, spot, lanes] = rate[c, spot, lanes] + more[c]
-                    next_ref[c, at, pl.ds(rows, TILE), lanes] = (
-                        next_ref[c, at, pl.ds(rows, TILE), lanes] - time_step * more[c]
-                    )
-        return carry
-
-    lax.fori_loop(0, tiles, mend, 0)
-
-    factor, shift = quotient(cells * width * groups, width * groups)
-    power = depth.bit_length() - 1
-    origin = block * (cells * width * groups)
+    along = ask[2:3, :]
+    first, last = along == 0.0, along == float(cells - 1)
+    more = [
+        jnp.where(first, scalar("ends", 2) * got[0, f:f + 1, :], 0.0)
+        + jnp.where(last, scalar("ends", 3) * got[1, f:f + 1, :], 0.0) for f in fields
+    ]
+    stream, flow = (jnp.where(first, own_ref[k:k + 1, :], own_ref[2 + k:3 + k, :]) for k in range(2))
+    mends[...] = jnp.zeros_like(mends)
+    for c, row in enumerate((
+        flow * more[0] + more[1], flow * more[1] + stream * more[4] + more[0], flow * more[2], flow * more[3],
+    )):
+        mends[c:c + 1, :] = row
+    mended = mends[...].T
 
     def pick(k, carry):
-        cell = cell_ref[k]
-        line = (cell >> power if depth & (depth - 1) == 0 else lax.div(cell, depth)) - origin
-        along_x = (line * factor) >> shift
-        along_y = jnp.clip(line - along_x * (width * groups) - group * width, 0, width - 1)
-        along_x = jnp.clip(along_x, 0, cells - 1)
-        row = along_x * width + along_y
+        row = lines[k]
         for c in range(4):
             picked[c, pl.ds(k, 1), :] = rate[c, pl.ds(row, 1), :]
-        picked[4, pl.ds(k, 1), :] = next_ref[0, along_x, pl.ds(along_y, 1), :]
         return carry
 
     lax.fori_loop(0, faces, pick, 0, unroll=4)
     mask = lax.broadcasted_iota(jnp.int32, (faces, depth), 1) == column(6).astype(jnp.int32)
-    at = [jnp.sum(jnp.where(mask, picked[c], 0.0), axis=1, keepdims=True) for c in range(5)]
-    normal_rate = normal[0] * at[1] + normal[1] * at[2] + normal[2] * at[3]
-    contribution[...] = at[4] * kernels[2] - at[0] * kernels[1] - normal_rate * kernels[0]
-
-    def gather(b, carry):
-        binned[pl.ds(b, 1), :] = jnp.sum(
-            jnp.where(bin_ref[...] == b, contribution[...], 0.0), axis=0, keepdims=True
-        )
-        return carry
-
-    lax.fori_loop(0, BINS, gather, 0, unroll=2)
+    at = [
+        jnp.sum(jnp.where(mask, picked[c], 0.0), axis=1, keepdims=True) + mended[0:faces, c:c + 1] for c in range(4)
+    ]
+    pressure = column(7) - time_step * at[0]
+    normal_rate = column(0) * at[1] + column(1) * at[2] + column(2) * at[3]
+    contribution[...] = pressure * kernels[2] - at[0] * kernels[1] - normal_rate * kernels[0]
+
+    def gather(k, carry):
+        b0 = pl.multiple_of(k * TILE, TILE)
+        for o in range(observers // LANES):
+            lanes = slice(o * LANES, (o + 1) * LANES)
+            totals = [jnp.zeros((TILE, LANES), jnp.float32)] * TILE
+            for r in range(0, faces, TILE):
+                bins, parts = bin_ref[r:r + TILE, lanes], contribution[r:r + TILE, lanes]
+                totals = [
+                    total + jnp.where(bins == b0 + j, parts, 0.0) for j, total in enumerate(totals)
+                ]
+            binned[pl.ds(b0, TILE), lanes] = jnp.concatenate(
+                [jnp.sum(total, axis=0, keepdims=True) for total in totals], axis=0
+            )
+        return carry
+
+    lax.fori_loop(0, BINS // TILE, gather, 0)
     share, beside = observers // count, LANES // BINS
     dense = share % (TILE * beside) == 0
     if not dense:
@@ -538,6 +617,27 @@
             device_id=target, device_id_type=MESH,
         ))
         copies[-1].start()
+    for entry in planes[0] + planes[1]:
+        arrive(*entry)
+
+    def mend(t, carry):
+        rows = first_row(t)
+        for at, plane, end in ((0, left_plane, 2), (cells - 1, right_plane, 3)):
+            spot = pl.ds(pl.multiple_of(at * width + rows, TILE), TILE)
+            for h in range(halves):
+                lanes = slice(h * LANES, (h + 1) * LANES)
+                px, ux, vx, wx, fx = (scalar("ends", end) * plane[f, pl.ds(rows, TILE), lanes] for f in fields)
+                stream, flow = value(1, at, rows, h), value(4, at, rows, h)
+                more = (flow * px + ux, flow * ux + stream * fx + px, flow * vx, flow * wx)
+                for c in range(4):
+                    rate[c, spot, lanes] = rate[c, spot, lanes] + more[c]
+                    next_ref[c, at, pl.ds(rows, TILE), lanes] = (
+                        next_ref[c, at, pl.ds(rows, TILE), lanes] - time_step * more[c]
+                    )
+        return carry
+
+    lax.fori_loop(0, tiles, mend, 0)
+
     total = pieces[me]
     for k in range(count - 1):
         copies[k].wait_recv()
@@ -553,7 +653,7 @@
 
     for k in range(count - 1):
         copies[k].wait_send()
-    for entry in halos + planes[0] + planes[1]:
+    for entry in halos + planes[0] + planes[1] + asks + replies:
         sent(*entry)
 
     def drain(t, carry):
@@ -609,11 +709,15 @@
         ] + [sums] * 8 + [
             VMEM((5, width, depth), f32), VMEM((5, width, depth), f32),
             VMEM((TILE, padded_faces), f32), VMEM((3, faces, observers), f32),
-            VMEM((5, faces, depth), f32), VMEM((faces, observers), f32),
+            VMEM((4, faces, depth), f32), VMEM((faces, observers), f32),
             VMEM((BINS, observers), f32), VMEM((devices,) + packed, f32),
             VMEM((devices - 1,) + packed, f32),
+            SMEM((faces,), jnp.int32), VMEM((halves, faces, LANES), f32), VMEM((TILE, padded_faces), f32), VMEM((2, TILE, padded_faces), f32),
+            VMEM((2, TILE, padded_faces), f32), VMEM((2, TILE, padded_faces), f32),
+            VMEM((TILE, padded_faces), f32), VMEM((padded_faces, TILE), f32), VMEM((TILE, padded_faces), f32),
             dma((len(PADDED) * halves + len(PLAIN) + 3,)), dma((2,)), dma((2,)), dma((2, 3)), dma((2, 3)),
             dma((4, tiles)), dma((4, tiles)), dma((devices - 1,)), dma((devices - 1,)),
+            dma((2,)), dma((2,)), dma((2,)), dma((2,)),
         ],
         compiler_params=pltpu.CompilerParams(
             collective_id=0, has_side_effects=True, vmem_limit_bytes=VMEM_MIB * 1024 * 1024

time: 49.1 us -> 40.7 us (0.83)
  Pallas kernels: 48.3 us -> 39.9 us
    pallas_call x1, Pallas kernels: 45.5 us -> 37.2 us  [per_device(): pl.pallas_call(functools.partial(fused_kernel, sizes, table.at, table.str...]
where the time goes in v2:
time: 40.7 us; the launch traced here: 40.6 us
  Pallas kernels  39.9 us (98%)
  between operations  0.64 us (2%)
    pallas_call x1, Pallas kernels, per_device(): pl.pallas_call(functools.partial(fused_kernel, sizes, table.at, table.str...  37.2 us
    pallas_call x1, Pallas kernels, per_device(): pl.pallas_call(copy_kernel, out_shape=(jax.ShapeDtypeStruct(state.shape,...  2.72 us

profile of v2, /device:TPU:0, one launch (start us, length us, event | category | flops | bytes accessed | tf_op | source)
XLA Modules:
  0.0 40.6 jit_solution(17302597159058009388)
XLA Ops:
  0.6 37.2 %shard_map.104 = (f32[4,32,48,256]{3,2,1,0:T(8,128)S(1)}, f32[16,64]{1,0:T(8,128)S(1)}) custom-call(f32[1728]{0:T(1024)} %constant.5.clone.table_ref, s32[192]{0:T(256)} %cell_ref.1, f32[4,32,48,256]{3,2,1,0:T(8,128)} %state_ref.1, f32[32,48,256]{2,1,0:T(8,128)} %flow_ref.1, bf16[256,256]{1,0:T(8,128)(2,1)} %constant.6.zhi_in, ...), custom_call_target="tpu_custom_call" | custom-call | tf_op jit(solution)/shard_map/pallas_call | solution.py:696
  37.8 2.7 %shard_map.105 = (f32[4,32,48,256]{3,2,1,0:T(8,128)}, f32[16,64]{1,0:T(8,128)}) custom-call(f32[4,32,48,256]{3,2,1,0:T(8,128)S(1)} %get-tuple-element.4.next_ref, f32[16,64]{1,0:T(8,128)S(1)} %get-tuple-element.5.signal_ref), custom_call_target="tpu_custom_call" | custom-call | tf_op jit(solution)/shard_map/pallas_call | solution.py:729

commit v3 on v2

--- a/solution.py
+++ b/solution.py
@@ -13,7 +13,7 @@
 LANES = 128
 REACH = 3
 VMEM_MIB = 54
-EARLY = ()
+EARLY = (0, 2)
 
 time_step = 0.25
 four_pi = 4.0 * 3.141592653589793
@@ -133,10 +133,10 @@
 
 def fused_kernel(
     sizes, where, stride,
-    table_ref, cell_ref, state_ref, flow_ref, zhi_in, zlo_in,
-    cells_ref, normal_ref, pos_ref, observer_ref, bin_in,
+    table_in, cell_in, state_ref, flow_ref, zhi_in, zlo_in,
+    cells_in, normal_in, pos_in, observer_in, bin_in,
     next_ref, signal_ref,
-    zhi_ref, zlo_ref, bin_ref, pad, plain, base, swept, rate,
+    table_ref, cell_ref, cells_ref, normal_ref, pos_ref, observer_ref, zhi_ref, zlo_ref, bin_ref, pad, plain, base, swept, rate,
     to_right, to_left, left_sum, right_sum, on_right, on_left, far_left, far_right,
     left_plane, right_plane,
     geometry, kernels, picked, contribution, binned, pieces, landing,
@@ -181,9 +181,12 @@
         loads.append(pltpu.make_async_copy(state_ref.at[f], plain.at[slot], load_sem.at[len(loads)]))
     spare = [
         pltpu.make_async_copy(source, target, load_sem.at[len(loads) + k])
-        for k, (source, target) in enumerate(((zhi_in, zhi_ref), (zlo_in, zlo_ref), (bin_in, bin_ref)))
+        for k, (source, target) in enumerate((
+            (cells_in, cells_ref), (table_in, table_ref), (cell_in, cell_ref), (zhi_in, zhi_ref), (zlo_in, zlo_ref),
+            (normal_in, normal_ref), (pos_in, pos_ref), (observer_in, observer_ref), (bin_in, bin_ref),
+        ))
     ]
-    for load in loads + spare:
+    for load in spare[:2] + loads + spare[2:]:
         load.start()
 
     barrier = pltpu.get_barrier_semaphore()
@@ -241,13 +244,14 @@
         (remote(pad.at[:, :, :, TILE:TILE + REACH, :], pad.at[:, :, :, TILE + width:TILE + width + REACH, :],
                 halo_send.at[1], halo_recv.at[1], "yz", -1), "yz", -1),
     ]
+    straight = lax.rem(block, 2)
     planes = [[], []]
     for side, (at, target, shift) in enumerate(((cells - 1, left_plane, 1), (0, right_plane, -1))):
         for piece, (source, into) in enumerate((
             (state_ref.at[0:2, at], target.at[0:2]), (state_ref.at[2:4, at], target.at[2:4]),
             (flow_ref.at[at], target.at[4]),
         )):
-            planes[0 if piece in EARLY else 1].append((remote(
+            planes[0 if piece in EARLY else 1].append((side, remote(
                 source, into, plane_send.at[side, piece], plane_recv.at[side, piece], "gx", shift
             ), "gx", shift))
 
@@ -268,6 +272,7 @@
         along_x = (line * factor) >> shift
         return along_x, line - along_x * (width * groups) - group * width
 
+    spare[0].wait()
     ask[...] = jnp.full_like(ask, -1.0)
     along_x, along_y = locate(cells_ref[...])
     along_z = cells_ref[...] & (depth - 1) if depth & (depth - 1) == 0 else lax.rem(cells_ref[...], depth)
@@ -285,13 +290,15 @@
     pl.semaphore_wait(barrier, count - 1)
     for entry in asks:
         start(*entry)
-    for entry in planes[0]:
-        start(*entry)
+    for side, *entry in planes[0]:
+        @pl.when(straight == side)
+        def _():
+            start(*entry)
     for load in loads[:len(PADDED) * halves]:
         load.wait()
     for entry in halos:
         start(*entry)
-    for load in loads[len(PADDED) * halves:] + spare:
+    for load in loads[len(PADDED) * halves:] + spare[1:2]:
         load.wait()
 
     fields = range(5)
@@ -325,6 +332,9 @@
         start(*near(0, t))
         start(*near(1, t))
 
+
+    for load in spare[2:]:
+        load.wait()
 
     together = 4 if cells % 4 == 0 else 1
 
@@ -534,9 +544,13 @@
         arrive(*near(0, t))
         arrive(*near(1, t))
 
-        @pl.when(t == max(tiles - 2, 0))
+        @pl.when(t == tiles - 1)
         def _():
-            for entry in planes[1]:
+            for side, *entry in planes[0]:
+                @pl.when(straight != side)
+                def _():
+                    start(*entry)
+            for side, *entry in planes[1]:
                 start(*entry)
 
         finish(t)
@@ -617,7 +631,7 @@
             device_id=target, device_id_type=MESH,
         ))
         copies[-1].start()
-    for entry in planes[0] + planes[1]:
+    for side, *entry in planes[0] + planes[1]:
         arrive(*entry)
 
     def mend(t, carry):
@@ -653,7 +667,7 @@
 
     for k in range(count - 1):
         copies[k].wait_send()
-    for entry in halos + planes[0] + planes[1] + asks + replies:
+    for entry in halos + [tuple(entry) for side, *entry in planes[0] + planes[1]] + asks + replies:
         sent(*entry)
 
     def drain(t, carry):
@@ -696,9 +710,11 @@
     state_next, signal = pl.pallas_call(
         functools.partial(fused_kernel, sizes, table.at, table.stride),
         out_shape=(VMEM(state.shape, f32), VMEM((share, BINS), f32)),
-        in_specs=[smem, smem, hbm, hbm, hbm, hbm, vmem, vmem, vmem, vmem, hbm],
+        in_specs=[hbm] * 11,
         out_specs=(vmem, vmem),
         scratch_shapes=[
+            SMEM(table.values.shape, f32), SMEM((faces,), jnp.int32), VMEM((1, faces), jnp.int32),
+            VMEM((3, faces), f32), VMEM((3, faces), f32), VMEM((3, observers), f32),
             VMEM((depth, depth), jnp.bfloat16), VMEM((depth, depth), jnp.bfloat16),
             VMEM((faces, observers), jnp.int32),
             VMEM((len(PADDED), halves, cells, width + 2 * TILE, LANES), f32),
@@ -715,7 +731,7 @@
             SMEM((faces,), jnp.int32), VMEM((halves, faces, LANES), f32), VMEM((TILE, padded_faces), f32), VMEM((2, TILE, padded_faces), f32),
             VMEM((2, TILE, padded_faces), f32), VMEM((2, TILE, padded_faces), f32),
             VMEM((TILE, padded_faces), f32), VMEM((padded_faces, TILE), f32), VMEM((TILE, padded_faces), f32),
-            dma((len(PADDED) * halves + len(PLAIN) + 3,)), dma((2,)), dma((2,)), dma((2, 3)), dma((2, 3)),
+            dma((len(PADDED) * halves + len(PLAIN) + 9,)), dma((2,)), dma((2,)), dma((2, 3)), dma((2, 3)),
             dma((4, tiles)), dma((4, tiles)), dma((devices - 1,)), dma((devices - 1,)),
             dma((2,)), dma((2,)), dma((2,)), dma((2,)),
         ],

time: 40.7 us -> 39.2 us (0.963)
  Pallas kernels: 39.9 us -> 38.4 us
    pallas_call x1, Pallas kernels: 37.2 us -> 35.7 us  [per_device(): pl.pallas_call(functools.partial(fused_kernel, sizes, table.at, table.str...]
where the time goes in v3:
time: 39.2 us; the launch traced here: 39.1 us
  Pallas kernels  38.4 us (98%)
  between operations  0.64 us (2%)
    pallas_call x1, Pallas kernels, per_device(): pl.pallas_call(functools.partial(fused_kernel, sizes, table.at, table.str...  35.7 us
    pallas_call x1, Pallas kernels, per_device(): pl.pallas_call(copy_kernel, out_shape=(jax.ShapeDtypeStruct(state.shape,...  2.72 us

profile of v3, /device:TPU:0, one launch (start us, length us, event | category | flops | bytes accessed | tf_op | source)
XLA Modules:
  0.0 39.1 jit_solution(6625378762268472003)
XLA Ops:
  0.6 35.7 %shard_map.104 = (f32[4,32,48,256]{3,2,1,0:T(8,128)S(1)}, f32[16,64]{1,0:T(8,128)S(1)}) custom-call(f32[1728]{0:T(1024)} %constant.5.clone.table_in, s32[192]{0:T(256)} %cell_in.1, f32[4,32,48,256]{3,2,1,0:T(8,128)} %state_ref.1, f32[32,48,256]{2,1,0:T(8,128)} %flow_ref.1, bf16[256,256]{1,0:T(8,128)(2,1)} %constant.6.zhi_in, ...), custom_call_target="tpu_custom_call" | custom-call | tf_op jit(solution)/shard_map/pallas_call | solution.py:710
  36.3 2.7 %shard_map.105 = (f32[4,32,48,256]{3,2,1,0:T(8,128)}, f32[16,64]{1,0:T(8,128)}) custom-call(f32[4,32,48,256]{3,2,1,0:T(8,128)S(1)} %get-tuple-element.4.next_ref, f32[16,64]{1,0:T(8,128)S(1)} %get-tuple-element.5.signal_ref), custom_call_target="tpu_custom_call" | custom-call | tf_op jit(solution)/shard_map/pallas_call | solution.py:745
